TPU v7x, 256 devices: a 4x2x16 block of a 4x16x16 slice. The times are simulated.
256 devices in a mesh: group: 2 (over y), ctx: 32 (over z, core), exp: 4 (over x).
Axes of the slice: x: 4, y: 2, z: 16, core: 2. Of those that a mesh axis runs over, the one named last changes fastest.
The devices are a block of a 4x16x16 slice.
Arguments:
- queries: bfloat16 [4096, 4096], P(('group', 'ctx'), 'exp'), parts along dimension 0, may hold values from -6 to 6
- new_keys: bfloat16 [4096, 1024], P(('group', 'ctx'), 'exp'), parts along dimension 0, may hold values from -6 to 6
- new_values: bfloat16 [4096, 1024], P(('group', 'ctx'), 'exp'), parts along dimension 0, may hold values from -6 to 6
- cache_keys: bfloat16 [16384, 1024], P(('group', 'ctx'), 'exp'), parts along dimension 0, may hold values from -6 to 6
- cache_values: bfloat16 [16384, 1024], P(('group', 'ctx'), 'exp'), parts along dimension 0, may hold values from -6 to 6
- offset: int32 [2], P('group'), parts along dimension 0, may hold values from 4096 to 8192
- token_ids: int32 [4096], P(('group', 'ctx')), parts along dimension 0, may hold values from 0 to 128255, as said below
- expert_table: int32 [256512], P('group'), parts along dimension 0, may hold values from 0 to 3
- norm_gain: float32 [4096], replicated, may hold values from 0.5 to 1.5
- w_gate: bfloat16 [4, 4096, 14336], P('exp', None, 'ctx'), may hold values from -0.09375 to 0.09375
- w_up: bfloat16 [4, 4096, 14336], P('exp', None, 'ctx'), may hold values from -0.09375 to 0.09375
- w_down: bfloat16 [4, 14336, 4096], P('exp', 'ctx'), may hold values from -0.046875 to 0.046875
Outputs:
- mixed: bfloat16 [4096, 4096], P(('group', 'ctx'), 'exp'), parts along dimension 0
There are 2 independent parts, one for each index of `group`. A program takes and returns all parts, laid end to end along the dimension named above; an argument that names none is the same for every part. Nothing has to cross between parts.
Inputs may be any that keep to these rules, and one draw needn't show every extreme that they name: Cache positions at or beyond offset are not yet filled. `token_ids`: in every block of 64 consecutive stretch tokens (one block per index of ctx) at most 32 tokens map to one expert through expert_table, and one expert takes exactly 32 tokens of every block.
All inputs are finite; a program needn't handle non-finite values.
Results may differ from a plain program's by a relative error of at most 0.025.
Values may be sent and summed in bfloat16 or wider, within the bound.
A program may use at most 128 MiB of HBM per device.

v0:
```python
import math
import jax
import jax.numpy as jnp
from jax import lax
from jax.sharding import Mesh
from jax.sharding import PartitionSpec as P

HEADS = 32
KV_HEADS = 8
HEAD_DIM = 128
CTX = ("ctx_0", "ctx_1")
GROUP_CTX = ("group", "ctx_0", "ctx_1")
masked_score = -1e30


def sent_together(arrays, axis, dim, along):
    widths = [a.shape[along] for a in arrays]
    both = jnp.concatenate(arrays, axis=along)
    filled = lax.all_gather(both, axis, axis=dim, tiled=True)
    return tuple(jnp.split(filled, [sum(widths[:k]) for k in range(1, len(widths))], axis=along))


def own_block(tiles, axes, order):
    shape = [lax.axis_size(a) for a in axes]
    tiles = tiles.reshape(*shape, *tiles.shape[1:])
    tiles = tiles.transpose(*order, *range(len(axes), tiles.ndim))
    tiles = tiles.reshape(-1, *tiles.shape[len(axes) :])
    for k in order:
        tiles = lax.psum_scatter(tiles, axes[k], scatter_dimension=0, tiled=True)
    return tiles[0]


def in_blocks(array, dim, devices):
    shape = array.shape
    tiles = array.reshape(*shape[:dim], devices, shape[dim] // devices, *shape[dim + 1 :])
    return jnp.moveaxis(tiles, dim, 0)


def summed_rows(array, axes, order, dim):
    devices = lax.axis_size(axes)
    return own_block(in_blocks(array, dim, devices), axes, order)


def split_heads(flat, heads):
    return flat.reshape(flat.shape[0], heads, flat.shape[1] // heads)


def partial_attend(query_rows, key_rows, value_rows, allowed):
    width = query_rows.shape[3]
    scores = jnp.einsum("rkgd,skd->rkgs", query_rows, key_rows, preferred_element_type=jnp.float32)
    scores = scores * (1.0 / math.sqrt(width))
    usable = allowed[:, None, None, :]
    peak = jnp.max(jnp.where(usable, scores, masked_score), axis=-1)
    unnorm = jnp.where(usable, jnp.exp(scores - peak[..., None]), 0.0)
    total = jnp.sum(unnorm, axis=-1)
    numer = jnp.einsum(
        "rkgs,skd->rkgd",
        unnorm.astype(jnp.bfloat16),
        value_rows,
        preferred_element_type=jnp.float32,
    )
    return (numer, peak, total)


def on_device(
    queries,
    new_keys,
    new_values,
    cache_keys,
    cache_values,
    offset,
    token_ids,
    expert_table,
    norm_gain,
    w_gate,
    w_up,
    w_down,
):
    owners = lax.axis_size("exp")
    heads_local = HEADS // owners
    kv_local = KV_HEADS // owners
    group = HEADS // KV_HEADS
    tok_count = queries.shape[0]
    cache_len = cache_keys.shape[0]
    shard = lax.axis_index(CTX)
    limit = offset[0]
    key_rows = jnp.concatenate([cache_keys, new_keys], axis=0)
    value_rows = jnp.concatenate([cache_values, new_values], axis=0)
    span = key_rows.shape[0]
    own_index = shard * tok_count + jnp.arange(tok_count, dtype=jnp.int32)
    grouped = queries.reshape(tok_count, kv_local, group, HEAD_DIM)
    piece_keys, piece_values = sent_together((key_rows, value_rows), CTX, 0, 1)
    flat = jnp.arange(piece_keys.shape[0], dtype=jnp.int32)
    source = flat // span
    inner = flat % span
    cache_ok = source * cache_len + inner < limit
    stretch_ok = (source * tok_count + inner - cache_len)[None, :] <= own_index[:, None]
    allowed = jnp.where((inner < cache_len)[None, :], cache_ok[None, :], stretch_ok)
    numer, peak, total = partial_attend(
        grouped, split_heads(piece_keys, kv_local), split_heads(piece_values, kv_local), allowed
    )
    best = jnp.full((tok_count, kv_local, group), masked_score, jnp.float32)
    higher = jnp.maximum(best, peak)
    fresh = jnp.exp(peak - higher)
    accum = numer * fresh[..., None]
    denom = total * fresh
    attended = (
        (accum / denom[..., None]).reshape(tok_count, heads_local * HEAD_DIM).astype(jnp.bfloat16)
    )
    capacity = tok_count // 2
    chosen = expert_table[token_ids]
    onehot = (chosen[:, None] == jnp.arange(owners, dtype=jnp.int32)[None, :]).astype(jnp.int32)
    earlier = jnp.cumsum(onehot, axis=0) - onehot
    slot = jnp.sum(earlier * onehot, axis=1)
    target = chosen * capacity + slot
    dispatch = (jnp.arange(owners * capacity, dtype=jnp.int32)[:, None] == target[None, :]).astype(
        jnp.bfloat16
    )
    packed = jnp.dot(dispatch, attended, preferred_element_type=jnp.float32).astype(jnp.bfloat16)
    arrived = lax.all_to_all(packed, "exp", split_axis=0, concat_axis=1, tiled=True)
    values32 = arrived.astype(jnp.float32)
    scale = lax.rsqrt(jnp.mean(values32 * values32, axis=-1, keepdims=True) + 1e-05)
    normed = (values32 * scale * norm_gain).astype(jnp.bfloat16)
    gate_w = w_gate[0]
    up_w = w_up[0]
    down_w = w_down[0]
    piece = lax.all_gather(normed, CTX, axis=0, tiled=True)
    gate = jnp.dot(piece, gate_w, preferred_element_type=jnp.float32)
    upper = jnp.dot(piece, up_w, preferred_element_type=jnp.float32)
    hidden = (jax.nn.silu(gate) * upper).astype(jnp.bfloat16)
    summed = summed_rows(
        jnp.dot(hidden, down_w, preferred_element_type=jnp.float32).astype(jnp.bfloat16),
        CTX,
        (1, 0),
        0,
    ).astype(jnp.float32)
    combined = (normed.astype(jnp.float32) + summed).astype(jnp.bfloat16)
    returned = lax.all_to_all(combined, "exp", split_axis=1, concat_axis=0, tiled=True)
    collect = (target[:, None] == jnp.arange(owners * capacity, dtype=jnp.int32)[None, :]).astype(
        jnp.bfloat16
    )
    return jnp.dot(collect, returned, preferred_element_type=jnp.float32).astype(jnp.bfloat16)


def solution(mesh):
    torus = Mesh(
        mesh.devices.reshape(mesh.shape["group"], 16, 2, mesh.shape["exp"]),
        ("group", "ctx_0", "ctx_1", "exp"),
    )
    placed = (
        P(GROUP_CTX, "exp"),
        P(GROUP_CTX, "exp"),
        P(GROUP_CTX, "exp"),
        P(GROUP_CTX, "exp"),
        P(GROUP_CTX, "exp"),
        P("group"),
        P(GROUP_CTX),
        P("group"),
        P(),
        P("exp", None, CTX),
        P("exp", None, CTX),
        P("exp", CTX, None),
    )
    return jax.shard_map(
        on_device, mesh=torus, in_specs=placed, out_specs=P(GROUP_CTX, "exp"), check_vma=False
    )
```

profile of v0, /device:TPU:40, one launch (start us, length us, event | category | flops | bytes accessed | tf_op | source)
XLA Modules:
  0.0 400.0 jit_solution(10660511344860597699)
XLA Ops:
  6.5 0.0 copy-start
  6.6 0.0 all-gather.3.cloned.1.call-start
  6.6 1.8 maximum_maximum_fusion
  8.4 0.1 all-gather.3.cloned.1.call-update
  8.4 0.1 all-gather.5.cloned.1.call-start
  9.2 1.0 reshape.150
  10.1 0.7 compare_select_fusion.1
  10.8 0.0 copy-done
  10.8 0.8 gather_fusion
  11.6 0.1 fusion.40
  11.7 0.1 reduce_window_sum.11
  11.8 0.2 select_reduce_fusion
  12.0 0.5 compare_select_fusion
  12.6 89.4 %all-gather.3.cloned.1.call-done = bf16[10240,512]{1,0:T(8,128)(2,1)} async-done(((bf16[320,512]{1,0:T(8,128)(2,1)}), bf16[10240,512]{1,0:T(8,128)(2,1)}) %all-gather.3.cloned.1.call-update) | async-done | bytes 10485776 | tf_op jit(solution)/shard_map/all_gather | solution.py:19
  102.0 8.9 %fusion.47 = (bf16[10240,256]{1,0:T(8,128)(2,1)}, bf16[10240,256]{1,0:T(8,128)(2,1)}) fusion(bf16[10240,512]{1,0:T(8,128)(2,1)} %all-gather.3.cloned.1.call-done), kind=kLoop, calls=%fused_computation.65 | loop fusion | bytes 20971520 | tf_op jit(solution)/shard_map/split | solution.py:20
  110.9 7.9 %copy.50 = bf16[10240,256]{0,1:T(8,128)(2,1)} copy(bf16[10240,256]{1,0:T(8,128)(2,1)} %get-tuple-element.6) | data formatting | bytes 10485760
  118.8 8.0 %copy.51 = bf16[10240,256]{0,1:T(8,128)(2,1)} copy(bf16[10240,256]{1,0:T(8,128)(2,1)} %get-tuple-element.5) | data formatting | bytes 10485760
  126.7 12.0 %fusion = (f32[64,2,4]{0,2,1:T(4,128)S(1)}, f32[2,10240,64,4]{1,2,3,0:T(8,128)}) fusion(pred[64,10240]{1,0:T(8,128)(4,1)S(1)} %compare_select_fusion, bf16[10240,2,128,1]{0,2,3,1:T(8,128)(2,1)} %bitcast.77, bf16[64,2,4,128]{3,2,1,0:T(4,128)(2,1)S(1)} %reshape.150), kind=kOutput, calls=%fused_computation.3 | convolution fusion | flops 1357905408 | bytes 27002880 | tf_op jit(solution)/shard_map/rkgd,skd->rkgs/dot_general | solution.py:50
  138.7 10.0 %fusion.3 = f32[64,2,4]{0,2,1:T(4,128)S(1)} fusion(f32[2,10240,64,4]{1,2,3,0:T(8,128)} %get-tuple-element.10, f32[64,2,4]{0,2,1:T(4,128)S(1)} %get-tuple-element.9, pred[64,10240]{1,0:T(8,128)(4,1)S(1)} %compare_select_fusion), kind=kLoop, calls=%fused_computation.6 | loop fusion | flops 20971008 | bytes 21630976 | tf_op jit(solution)/shard_map/reduce_sum | solution.py:55
  148.7 0.0 copy-start.2
  148.7 10.6 %fusion.26 = bf16[64,2,4,128]{3,0,2,1:T(8,128)(2,1)S(1)} fusion(bf16[10240,2,128,1]{0,2,3,1:T(8,128)(2,1)} %bitcast.79, f32[2,10240,64,4]{1,2,3,0:T(8,128)} %get-tuple-element.10, f32[64,2,4]{0,2,1:T(4,128)S(1)} %get-tuple-element.9, pred[64,10240]{1,0:T(8,128)(4,1)S(1)} %compare_select_fusion, f32[64,2,4]{0,2,1:T(4,128)S(1)} %get-tuple-element.8, ...), kind=kOutput, calls=%fused_computation.23 | convolution fusion | flops 1363345408 | bytes 27006976 | tf_op jit(solution)/shard_map/rkgs,skd->rkgd/dot_general | solution.py:56
  159.4 0.1 copy.40
  159.5 0.1 convert_element_type.62
  159.6 0.2 convolution_convert_fusion.1
  159.8 11.1 %all_to_all.29 = bf16[4,32,1024]{2,1,0:T(8,128)(2,1)S(1)} all-to-all(bf16[4,32,1024]{2,1,0:T(8,128)(2,1)S(1)} %bitcast.83), channel_id=1, replica_groups=mesh['group'=2,'ctx_0'=16,'ctx_1'=2,'exp'=4] {'exp'}, dimensions={0} | all-to-all | bytes 524288 | tf_op jit(solution)/shard_map/all_to_all | solution.py:120
  170.9 0.2 copy_convert_fusion
  171.1 0.3 copy.52
  171.4 0.4 multiply_reduce_fusion
  171.8 0.0 copy-done.2
  171.8 0.8 multiply_convert_fusion.1
  172.6 0.1 all-gather.5.cloned.1.call-update
  172.7 0.2 reduce-scatter.3.cloned.1.call-start
  172.9 71.4 %all-gather.5.cloned.1.call-done = bf16[1024,4096]{1,0:T(8,128)(2,1)} async-done(((bf16[32,4096]{1,0:T(8,128)(2,1)}), bf16[1024,4096]{1,0:T(8,128)(2,1)}) %all-gather.5.cloned.1.call-update) | async-done | bytes 8388624 | tf_op jit(solution)/shard_map/all_gather | solution.py:127
  244.3 7.5 %fusion.11 = f32[1024,448]{0,1:T(8,128)S(1)} fusion(bf16[1024,4096]{1,0:T(8,128)(2,1)} %all-gather.5.cloned.1.call-done, bf16[1,4096,448]{1,2,0:T(8,128)(2,1)} %param.21), kind=kOutput, calls=%fused_computation.14 | convolution fusion | flops 3758096384 | bytes 13893632 | tf_op jit(solution)/shard_map/dot_general | solution.py:128
  251.8 15.2 %convolution_convert_fusion = bf16[1024,4096]{1,0:T(8,128)(2,1)} fusion(bf16[1,448,4096]{2,1,0:T(8,128)(2,1)} %param.23, f32[1024,448]{0,1:T(8,128)S(1)} %fusion.11, bf16[1024,4096]{1,0:T(8,128)(2,1)} %all-gather.5.cloned.1.call-done, bf16[1,4096,448]{1,2,0:T(8,128)(2,1)} %param.22), kind=kOutput, calls=%fused_computation.10 | convolution fusion | flops 7523139584 | bytes 25952256 | tf_op jit(solution)/shard_map/dot_general | solution.py:132
  267.0 7.7 %copy.42 = bf16[16,2,32,4096]{3,2,0,1:T(8,128)(2,1)} copy(bf16[16,2,32,4096]{3,2,1,0:T(8,128)(2,1)} %bitcast.78) | data formatting | bytes 16777216 | tf_op jit(solution)/shard_map/reshape;reshape | solution.py:25
  274.8 0.1 reduce-scatter.3.cloned.1.call-update
  274.8 0.0 copy-start.1
  274.8 0.1 reduce-scatter.5.cloned.1.call-start
  274.9 22.1 %reduce-scatter.3.cloned.1.call-done = bf16[16,32,4096]{2,1,0:T(8,128)(2,1)} async-done(((bf16[32,32,4096]{2,1,0:T(8,128)(2,1)}), bf16[16,32,4096]{2,1,0:T(8,128)(2,1)}) %reduce-scatter.3.cloned.1.call-update) | async-done | bytes 4194320 | tf_op jit(solution)/shard_map/reduce_scatter | solution.py:29
  297.0 0.1 reduce-scatter.5.cloned.1.call-update
  297.1 82.6 %reduce-scatter.5.cloned.1.call-done = bf16[1,32,4096]{2,1,0:T(8,128)(2,1)} async-done(((bf16[16,32,4096]{2,1,0:T(8,128)(2,1)}), bf16[1,32,4096]{2,1,0:T(8,128)(2,1)}) %reduce-scatter.5.cloned.1.call-update) | async-done | bytes 262160 | tf_op jit(solution)/shard_map/reduce_scatter | solution.py:29
  379.7 1.4 reshape.153
  381.1 0.3 fusion.30
  381.4 0.1 copy.43
  381.4 11.2 %all_to_all.30 = bf16[32,4,1024]{2,0,1:T(8,128)(2,1)S(1)} all-to-all(bf16[32,4,1024]{2,0,1:T(8,128)(2,1)S(1)} %copy.43), channel_id=1, replica_groups=mesh['group'=2,'ctx_0'=16,'ctx_1'=2,'exp'=4] {'exp'}, dimensions={1} | all-to-all | bytes 524288 | tf_op jit(solution)/shard_map/all_to_all | solution.py:138
  392.6 0.9 convolution_convert_fusion.2
  393.5 0.0 copy-done.1
  (8 shorter events, 0.1 us)
Async XLA Ops:
  6.5 4.3 %copy-start = (s32[128256]{0:T(1024)S(1)}, s32[128256]{0:T(1024)}, u32[]{:S(2)}) copy-start(s32[128256]{0:T(1024)} %param.19) | copy-start | bytes 1539076
  6.6 95.5 %all-gather.3.cloned.1.call-start = ((), (), s32[]{:S(2)}) async-start(), calls=%async_computation.4 | async-start | bytes 10813440 | tf_op jit(solution)/shard_map/all_gather | solution.py:19
  8.4 235.9 %all-gather.5.cloned.1.call-start = ((), (), s32[]{:S(2)}) async-start(), calls=%async_computation.5 | async-start | bytes 8650752 | tf_op jit(solution)/shard_map/all_gather | solution.py:127
  148.7 23.0 %copy-start.2 = (f32[4096]{0:T(1024)S(1)}, f32[4096]{0:T(1024)}, u32[]{:S(2)}) copy-start(f32[4096]{0:T(1024)} %param.20) | copy-start | bytes 49156
  172.7 124.3 %reduce-scatter.3.cloned.1.call-start = ((), (), s32[]{:S(2)}) async-start(), calls=%async_computation.6 | async-start | bytes 12582912 | tf_op jit(solution)/shard_map/reduce_scatter | solution.py:29
  274.8 118.7 %copy-start.1 = (s32[128256]{0:T(1024)S(1)}, s32[128256]{0:T(1024)}, u32[]{:S(2)}) copy-start(s32[128256]{0:T(1024)} %param.19) | copy-start | bytes 1539076
  274.8 104.9 %reduce-scatter.5.cloned.1.call-start = ((), (), s32[]{:S(2)}) async-start(), calls=%async_computation.7 | async-start | bytes 4456448 | tf_op jit(solution)/shard_map/reduce_scatter | solution.py:29
Sparse Core Ops, SparseCore 0:
  9.2 92.7 all-gather.2
  172.8 71.4 all-gather.4
  274.9 22.0 reduce-scatter.2
  299.4 80.2 reduce-scatter.4
where the time goes:
time: 401 us; the launch traced here: 400 us
  waiting for transfers between devices  266 us (66%)
  matrix products  46.4 us (12%)
  local copies, waits for them, and re-layouts  36.1 us (9%)
  blocking collectives  22.3 us (6%)
  other arithmetic  15.2 us (4%)
  between operations  13.9 us (3%)
    reduce_scatter x2, waiting for transfers between devices, own_block(): tiles = lax.psum_scatter(tiles, axes[k], scatter_dimension=0, tiled=True)  105 us
    all_gather x1, waiting for transfers between devices, sent_together(): filled = lax.all_gather(both, axis, axis=dim, tiled=True)  89.4 us
    all_gather x1, waiting for transfers between devices, on_device(): piece = lax.all_gather(normed, CTX, axis=0, tiled=True)  71.4 us
    unnamed x9, local copies, waits for them, and re-layouts  16.2 us
    dot_general x1, matrix products, on_device(): jnp.dot(hidden, down_w, preferred_element_type=jnp.float32)  15.2 us
    dot_general x1, matrix products, partial_attend(): jnp.einsum('rkgd,skd->rkgs', query_rows, key_rows, preferred_element_type...  12 us
    all_to_all x1, blocking collectives, on_device(): lax.all_to_all(combined, 'exp', split_axis=1, concat_axis=0, tiled=True)  11.2 us
    all_to_all x1, blocking collectives, on_device(): lax.all_to_all(packed, 'exp', split_axis=0, concat_axis=1, tiled=True)  11.1 us
  transfers between devices with their start and end apart: 4, of which 4 were waited for; matrix products, arithmetic and copies ran while one was open for 1% of the time, Pallas kernels for 0%

commit v1 on v0

--- a/solution.py
+++ b/solution.py
@@ -124,7 +124,9 @@
     gate_w = w_gate[0]
     up_w = w_up[0]
     down_w = w_down[0]
-    piece = lax.all_gather(normed, CTX, axis=0, tiled=True)
+    piece = jnp.concatenate(
+        lax.all_to_all(jnp.stack([normed] * lax.axis_size(CTX)), CTX, 0, 0), axis=0
+    )
     gate = jnp.dot(piece, gate_w, preferred_element_type=jnp.float32)
     upper = jnp.dot(piece, up_w, preferred_element_type=jnp.float32)
     hidden = (jax.nn.silu(gate) * upper).astype(jnp.bfloat16)

time: 401 us -> 701 us (1.75)
  blocking collectives: 22.3 us -> 401 us
  waiting for transfers between devices: 266 us -> 188 us
    all_to_all x0 -> x1, blocking collectives: none -> 378 us  [on_device(): lax.all_to_all(jnp.stack([normed] * lax.axis_size(CTX)), CTX, 0, 0)]
    all_gather x1 -> x0, waiting for transfers between devices: 71.4 us -> none  [on_device(): piece = lax.all_gather(normed, CTX, axis=0, tiled=True)]
    unnamed x9 -> x13, local copies, waits for them, and re-layouts: 16.2 us -> 19.4 us
  transfers between devices with their start and end apart: 4 -> 3, of which waited for: 4 -> 3; matrix products, arithmetic and copies ran while one was open for 1% -> 0% of each run, Pallas kernels for 0% -> 0%
where the time goes in v1:
time: 701 us; the launch traced here: 700 us
  blocking collectives  401 us (57%)
  waiting for transfers between devices  188 us (27%)
  matrix products  42.9 us (6%)
  local copies, waits for them, and re-layouts  40.4 us (6%)
  other arithmetic  14.5 us (2%)
  between operations  13.9 us (2%)
    all_to_all x1, blocking collectives, on_device(): lax.all_to_all(jnp.stack([normed] * lax.axis_size(CTX)), CTX, 0, 0)  378 us
    reduce_scatter x2, waiting for transfers between devices, own_block(): tiles = lax.psum_scatter(tiles, axes[k], scatter_dimension=0, tiled=True)  98 us
    all_gather x1, waiting for transfers between devices, sent_together(): filled = lax.all_gather(both, axis, axis=dim, tiled=True)  89.4 us
    unnamed x13, local copies, waits for them, and re-layouts  19.4 us
    dot_general x1, matrix products, on_device(): jnp.dot(hidden, down_w, preferred_element_type=jnp.float32)  15.2 us
  transfers between devices with their start and end apart: 3, of which 3 were waited for; matrix products, arithmetic and copies ran while one was open for 0% of the time, Pallas kernels for 0%

profile of v1, /device:TPU:40, one launch (start us, length us, event | category | flops | bytes accessed | tf_op | source)
XLA Modules:
  0.0 700.0 jit_solution(10354800393402841174)
XLA Ops:
  6.5 0.0 copy-start
  6.6 0.0 all-gather.2.cloned.1.call-start
  6.6 1.8 maximum_maximum_fusion
  8.4 0.1 all-gather.2.cloned.1.call-update
  8.4 0.1 reduce-scatter.3.cloned.1.call-start
  9.2 1.0 reshape.170
  10.1 0.7 compare_select_fusion.1
  10.8 0.0 copy-done
  10.8 0.8 gather_fusion
  11.6 0.1 fusion.40
  11.7 0.1 reduce_window_sum.11
  11.8 0.2 select_reduce_fusion
  12.0 0.5 compare_select_fusion
  12.6 89.4 %all-gather.2.cloned.1.call-done = bf16[10240,512]{1,0:T(8,128)(2,1)} async-done(((bf16[320,512]{1,0:T(8,128)(2,1)}), bf16[10240,512]{1,0:T(8,128)(2,1)}) %all-gather.2.cloned.1.call-update) | async-done | bytes 10485776 | tf_op jit(solution)/shard_map/all_gather | solution.py:19
  102.0 8.9 %fusion.47 = (bf16[10240,256]{1,0:T(8,128)(2,1)}, bf16[10240,256]{1,0:T(8,128)(2,1)}) fusion(bf16[10240,512]{1,0:T(8,128)(2,1)} %all-gather.2.cloned.1.call-done), kind=kLoop, calls=%fused_computation.65 | loop fusion | bytes 20971520 | tf_op jit(solution)/shard_map/split | solution.py:20
  110.9 7.9 %copy.50 = bf16[10240,256]{0,1:T(8,128)(2,1)} copy(bf16[10240,256]{1,0:T(8,128)(2,1)} %get-tuple-element.6) | data formatting | bytes 10485760
  118.8 8.0 %copy.51 = bf16[10240,256]{0,1:T(8,128)(2,1)} copy(bf16[10240,256]{1,0:T(8,128)(2,1)} %get-tuple-element.5) | data formatting | bytes 10485760
  126.7 12.0 %fusion = (f32[64,2,4]{0,2,1:T(4,128)S(1)}, f32[2,10240,64,4]{1,2,3,0:T(8,128)}) fusion(pred[64,10240]{1,0:T(8,128)(4,1)S(1)} %compare_select_fusion, bf16[10240,2,128,1]{0,2,3,1:T(8,128)(2,1)} %bitcast.78, bf16[64,2,4,128]{3,2,1,0:T(4,128)(2,1)S(1)} %reshape.170), kind=kOutput, calls=%fused_computation.3 | convolution fusion | flops 1357905408 | bytes 27002880 | tf_op jit(solution)/shard_map/rkgd,skd->rkgs/dot_general | solution.py:50
  138.7 10.0 %fusion.3 = f32[64,2,4]{0,2,1:T(4,128)S(1)} fusion(f32[2,10240,64,4]{1,2,3,0:T(8,128)} %get-tuple-element.10, f32[64,2,4]{0,2,1:T(4,128)S(1)} %get-tuple-element.9, pred[64,10240]{1,0:T(8,128)(4,1)S(1)} %compare_select_fusion), kind=kLoop, calls=%fused_computation.6 | loop fusion | flops 20971008 | bytes 21630976 | tf_op jit(solution)/shard_map/reduce_sum | solution.py:55
  148.7 0.0 copy-start.3
  148.7 10.6 %fusion.26 = bf16[64,2,4,128]{3,0,2,1:T(8,128)(2,1)S(1)} fusion(bf16[10240,2,128,1]{0,2,3,1:T(8,128)(2,1)} %bitcast.82, f32[2,10240,64,4]{1,2,3,0:T(8,128)} %get-tuple-element.10, f32[64,2,4]{0,2,1:T(4,128)S(1)} %get-tuple-element.9, pred[64,10240]{1,0:T(8,128)(4,1)S(1)} %compare_select_fusion, f32[64,2,4]{0,2,1:T(4,128)S(1)} %get-tuple-element.8, ...), kind=kOutput, calls=%fused_computation.23 | convolution fusion | flops 1363345408 | bytes 27006976 | tf_op jit(solution)/shard_map/rkgs,skd->rkgd/dot_general | solution.py:56
  159.4 0.1 copy.40
  159.5 0.1 convert_element_type.66
  159.6 0.2 convolution_convert_fusion.1
  159.8 11.1 %all_to_all.34 = bf16[4,32,1024]{2,1,0:T(8,128)(2,1)S(1)} all-to-all(bf16[4,32,1024]{2,1,0:T(8,128)(2,1)S(1)} %bitcast.86), channel_id=1, replica_groups=mesh['group'=2,'ctx_0'=16,'ctx_1'=2,'exp'=4] {'exp'}, dimensions={0} | all-to-all | bytes 524288 | tf_op jit(solution)/shard_map/all_to_all | solution.py:120
  170.9 0.2 copy_convert_fusion
  171.1 0.3 copy.52
  171.4 0.4 multiply_reduce_fusion
  171.8 0.0 copy-done.3
  171.8 0.1 multiply_convert_fusion.1
  171.9 1.0 stack.2
  172.9 0.0 copy-start.4
  172.9 378.1 %all_to_all.35 = bf16[32,32,4096]{2,1,0:T(8,128)(2,1)S(1)} all-to-all(bf16[32,32,4096]{2,1,0:T(8,128)(2,1)S(1)} %stack.2), channel_id=1, replica_groups=mesh['group'=2,'ctx_0'=16,'ctx_1'=2,'exp'=4] {'ctx_0','ctx_1'}, dimensions={0} | all-to-all | bytes 16777216 | tf_op jit(solution)/shard_map/all_to_all | solution.py:128
  551.1 0.0 copy-start.2
  551.1 3.2 copy-done.2
  554.3 0.0 copy-done.4
  554.3 4.0 fusion.11
  558.3 15.2 %convolution_convert_fusion = bf16[1024,4096]{1,0:T(8,128)(2,1)} fusion(bf16[1,448,4096]{2,1,0:T(8,128)(2,1)} %param.23, f32[1024,448]{0,1:T(8,128)S(1)} %fusion.11, bf16[1024,4096]{1,0:T(8,128)(2,1)} %bitcast.80, bf16[1,4096,448]{1,2,0:T(8,128)(2,1)} %param.22), kind=kOutput, calls=%fused_computation.10 | convolution fusion | flops 7523139584 | bytes 25952256 | tf_op jit(solution)/shard_map/dot_general | solution.py:134
  573.5 7.7 %copy.42 = bf16[16,2,32,4096]{3,2,0,1:T(8,128)(2,1)} copy(bf16[16,2,32,4096]{3,2,1,0:T(8,128)(2,1)} %bitcast.81) | data formatting | bytes 16777216 | tf_op jit(solution)/shard_map/reshape;reshape | solution.py:25
  581.2 0.1 reduce-scatter.3.cloned.1.call-update
  581.3 0.0 copy-start.1
  581.3 0.1 reduce-scatter.5.cloned.1.call-start
  581.4 15.4 %reduce-scatter.3.cloned.1.call-done = bf16[16,32,4096]{2,1,0:T(8,128)(2,1)} async-done(((bf16[32,32,4096]{2,1,0:T(8,128)(2,1)}), bf16[16,32,4096]{2,1,0:T(8,128)(2,1)}) %reduce-scatter.3.cloned.1.call-update) | async-done | bytes 4194320 | tf_op jit(solution)/shard_map/reduce_scatter | solution.py:29
  596.8 0.1 reduce-scatter.5.cloned.1.call-update
  596.8 82.6 %reduce-scatter.5.cloned.1.call-done = bf16[1,32,4096]{2,1,0:T(8,128)(2,1)} async-done(((bf16[16,32,4096]{2,1,0:T(8,128)(2,1)}), bf16[1,32,4096]{2,1,0:T(8,128)(2,1)}) %reduce-scatter.5.cloned.1.call-update) | async-done | bytes 262160 | tf_op jit(solution)/shard_map/reduce_scatter | solution.py:29
  679.5 1.4 reshape.174
  680.9 0.3 fusion.30
  681.2 0.1 copy.43
  681.3 11.3 %all_to_all.36 = bf16[32,4,1024]{2,0,1:T(8,128)(2,1)S(1)} all-to-all(bf16[32,4,1024]{2,0,1:T(8,128)(2,1)S(1)} %copy.43), channel_id=1, replica_groups=mesh['group'=2,'ctx_0'=16,'ctx_1'=2,'exp'=4] {'exp'}, dimensions={1} | all-to-all | bytes 524288 | tf_op jit(solution)/shard_map/all_to_all | solution.py:140
  692.6 0.9 convolution_convert_fusion.2
  693.4 0.0 copy-done.1
  (8 shorter events, 0.1 us)
Async XLA Ops:
  6.5 4.3 copy-start
  6.6 95.5 %all-gather.2.cloned.1.call-start = ((), (), s32[]{:S(2)}) async-start(), calls=%async_computation.5 | async-start | bytes 10813440 | tf_op jit(solution)/shard_map/all_gather | solution.py:19
  8.4 588.3 %reduce-scatter.3.cloned.1.call-start = ((), (), s32[]{:S(2)}) async-start(), calls=%async_computation.6 | async-start | bytes 12582912 | tf_op jit(solution)/shard_map/reduce_scatter | solution.py:29
  148.7 23.0 %copy-start.3 = (f32[4096]{0:T(1024)S(1)}, f32[4096]{0:T(1024)}, u32[]{:S(2)}) copy-start(f32[4096]{0:T(1024)} %param.20) | copy-start | bytes 49156
  172.9 381.4 %copy-start.4 = (bf16[1,4096,448]{1,2,0:T(8,128)(2,1)S(1)}, bf16[1,4096,448]{1,2,0:T(8,128)(2,1)}, u32[]{:S(2)}) copy-start(bf16[1,4096,448]{1,2,0:T(8,128)(2,1)} %param.21) | copy-start | bytes 11010052
  551.1 3.2 copy-start.2
  581.3 112.2 %copy-start.1 = (s32[128256]{0:T(1024)S(1)}, s32[128256]{0:T(1024)}, u32[]{:S(2)}) copy-start(s32[128256]{0:T(1024)} %param.19) | copy-start | bytes 1539076
  581.3 98.2 %reduce-scatter.5.cloned.1.call-start = ((), (), s32[]{:S(2)}) async-start(), calls=%async_computation.7 | async-start | bytes 4456448 | tf_op jit(solution)/shard_map/reduce_scatter | solution.py:29
Sparse Core Ops, SparseCore 0:
  9.2 92.7 all-gather.1
  581.4 15.3 reduce-scatter.2
  599.3 80.0 reduce-scatter.4
